TPU v7x, 64 devices: a 2x2x8 block of a 4x4x8 slice. The times are simulated.
64 devices in a mesh: batch: 4 (over x, y), dap: 16 (over z, core).
Axes of the slice: x: 2, y: 2, z: 8, core: 2. Of those that a mesh axis runs over, the one named last changes fastest.
The devices are a block of a 4x4x8 slice.
Arguments:
- pair: bfloat16 [1536, 384, 128], P(('batch', 'dap')), parts along dimension 0
- pair_mask: int32 [1536, 384], P(('batch', 'dap')), parts along dimension 0
- ln_in: bfloat16 [2, 2, 128], replicated
- w_proj: bfloat16 [2, 128, 512], replicated
- b_proj: bfloat16 [2, 512], replicated
- w_gate: bfloat16 [2, 128, 128], replicated
- b_gate: bfloat16 [2, 128], replicated
- ln_out: bfloat16 [2, 2, 128], replicated
- w_out: bfloat16 [2, 128, 128], replicated
- b_out: bfloat16 [2, 128], replicated
Outputs:
- output: bfloat16 [1536, 384, 128], P(('batch', 'dap')), parts along dimension 0
There are 4 independent parts. A program takes and returns all parts, laid end to end along the dimension named above; an argument that names none is the same for every part.
All inputs are finite; a program needn't handle non-finite values.
Results may differ from a plain program's by a relative error of at most 0.00397731.
Values are sent between devices in bfloat16 or wider.
A program may use at most 768 MiB of HBM per device.

v0:
```python
import jax
import jax.numpy as jnp
from jax import lax
from jax.sharding import PartitionSpec as P, NamedSharding

LN_EPS = 1e-5


def norm_last(values, scale, offset):
    centred = values - jnp.mean(values, axis=-1, keepdims=True)
    variance = jnp.mean(centred * centred, axis=-1, keepdims=True)
    return centred * lax.rsqrt(variance + LN_EPS) * scale.astype(jnp.float32) + offset.astype(jnp.float32)


def norm_channels(values, scale, offset):
    centred = values - jnp.mean(values, axis=-3, keepdims=True)
    variance = jnp.mean(centred * centred, axis=-3, keepdims=True)
    return (centred * lax.rsqrt(variance + LN_EPS) * scale.astype(jnp.float32)[:, None, None]
            + offset.astype(jnp.float32)[:, None, None])


def gated_side(projected, keep_mask, channels):
    return (keep_mask * jax.nn.sigmoid(projected[channels:2 * channels]) * projected[:channels]).astype(jnp.bfloat16)


def normalize_project(pair, keep_mask, ln_in, w_proj, b_proj, channels):
    normed = norm_last(pair.astype(jnp.float32), ln_in[0], ln_in[1]).astype(jnp.bfloat16)
    projected = jnp.einsum("zc,ijz->cij", w_proj, normed, preferred_element_type=jnp.float32)
    projected = projected + b_proj.astype(jnp.float32)[:, None, None]
    left = gated_side(projected[:2 * channels], keep_mask, channels)
    right = gated_side(projected[2 * channels:], keep_mask, channels)
    return normed, left, right


def finish_layer(pair, normed, tri_sum, w_gate, b_gate, ln_out, w_out, b_out):
    tri_norm = norm_channels(tri_sum, ln_out[0], ln_out[1]).astype(jnp.bfloat16)
    update = jnp.einsum("cij,cz->ijz", tri_norm, w_out, preferred_element_type=jnp.float32) + b_out.astype(jnp.float32)
    gates = jax.nn.sigmoid(jnp.einsum("ijz,zy->ijy", normed, w_gate, preferred_element_type=jnp.float32) + b_gate.astype(jnp.float32))
    return (pair.astype(jnp.float32) + gates * update).astype(jnp.bfloat16)


def solution(mesh):
    row_spec = P(("batch", "dap"), None, None)
    mask_spec = P(("batch", "dap"), None)

    def local_layers(pair, pair_mask, ln_in, w_proj, b_proj, w_gate, b_gate, ln_out, w_out, b_out):
        channels = w_out.shape[1]
        keep_mask = pair_mask.astype(jnp.float32)[None]
        normed, left, right = normalize_project(pair, keep_mask, ln_in[0], w_proj[0], b_proj[0], channels)
        right_all = lax.all_gather(right, "dap", axis=1, tiled=True)
        tri_sum = jnp.einsum("cik,cjk->cij", left, right_all, preferred_element_type=jnp.float32)
        first = finish_layer(pair, normed, tri_sum, w_gate[0], b_gate[0], ln_out[0], w_out[0], b_out[0])
        normed, left, right = normalize_project(first, keep_mask, ln_in[1], w_proj[1], b_proj[1], channels)
        left_cols = lax.all_to_all(left, "dap", 2, 1, tiled=True)
        right_all = lax.all_gather(right, "dap", axis=1, tiled=True)
        tri_sum = jnp.einsum("cki,ckj->cij", left_cols, right_all, preferred_element_type=jnp.float32)
        return finish_layer(first, normed, tri_sum, w_gate[1], b_gate[1], ln_out[1], w_out[1], b_out[1])

    return jax.shard_map(local_layers, mesh=mesh,
                         in_specs=(row_spec, mask_spec, P(), P(), P(), P(), P(), P(), P(), P()),
                         out_specs=row_spec, check_vma=False)
```

profile of v0, /device:TPU:21, one launch (start us, length us, event | category | flops | bytes accessed | tf_op | source)
XLA Modules:
  0.0 572.2 jit_solution(722229392783120170)
XLA Ops:
  6.6 0.1 all-gather.3.cloned.1.call-start
  6.6 3.0 copy.63
  9.7 0.4 convert_reduce_fusion.1
  10.1 0.7 fusion.12
  10.8 0.0 copy-done.7
  10.8 0.0 copy-done.6
  10.8 0.0 copy-done.5
  10.9 0.0 copy-done.3
  10.9 3.0 add_bitcast_fusion.1
  13.9 4.1 fusion.28
  17.9 4.3 copy.67
  22.3 0.1 all-gather.3.cloned.1.call-update
  22.3 0.2 all-gather.5.cloned.1.call-start
  22.6 4.5 copy.68
  27.0 0.0 copy-done.8
  27.0 0.0 copy-done.9
  27.0 0.0 copy-done.10
  27.1 191.2 %all-gather.3.cloned.1.call-done = bf16[128,384,384]{2,0,1:T(8,128)(2,1)} async-done(((bf16[128,24,384]{2,0,1:T(8,128)(2,1)}), bf16[128,384,384]{2,0,1:T(8,128)(2,1)}) %all-gather.3.cloned.1.call-update) | async-done | bytes 37748752 | tf_op jit(solution)/shard_map/all_gather | solution.py:50
  218.3 39.1 %fusion.58 = (f32[24,384]{1,0:T(8,128)S(1)}, f32[128,24,384]{2,1,0:T(8,128)}) fusion(bf16[128,24,384]{2,1,0:T(8,128)(2,1)} %copy.68, bf16[128,384,384]{2,0,1:T(8,128)(2,1)} %all-gather.3.cloned.1.call-done), kind=kOutput, calls=%fused_computation.96 | convolution fusion | flops 907140096 | bytes 44863488 | tf_op jit(solution)/shard_map/cik,cjk->cij/dot_general | solution.py:51
  257.3 0.0 copy-start
  257.4 3.0 multiply_reduce_fusion.1
  260.4 0.7 copy-done
  261.1 0.8 add_convert_fusion.1
  261.9 0.0 copy-done.4
  261.9 0.0 copy-start.11
  261.9 0.8 fusion.40
  262.7 0.0 copy-done.11
  262.7 3.0 convert_reduce_fusion
  265.8 0.0 copy-start.1
  265.8 0.7 fusion.8
  266.5 3.0 add_bitcast_fusion
  269.6 0.0 copy-done.1
  269.6 3.7 fusion.18
  273.3 4.3 copy.78
  277.5 0.1 all-gather.5.cloned.1.call-update
  277.6 1.5 copy.75
  279.1 86.5 %all_to_all.18 = bf16[128,24,384]{0,1,2:T(8,128)(2,1)S(1)} all-to-all(bf16[128,24,384]{0,1,2:T(8,128)(2,1)S(1)} %copy.75), channel_id=1, replica_groups=mesh['batch'=4,'dap'=16] {'dap'}, dimensions={2} | all-to-all | bytes 4718592 | tf_op jit(solution)/shard_map/all_to_all | solution.py:54
  365.7 1.9 copy.77
  367.6 3.7 copy.79
  371.3 146.2 %all-gather.5.cloned.1.call-done = bf16[128,384,384]{2,0,1:T(8,128)(2,1)} async-done(((bf16[128,24,384]{2,0,1:T(8,128)(2,1)}), bf16[128,384,384]{2,0,1:T(8,128)(2,1)}) %all-gather.5.cloned.1.call-update) | async-done | bytes 37748752 | tf_op jit(solution)/shard_map/all_gather | solution.py:55
  517.5 39.4 %fusion.59 = (f32[24,384]{1,0:T(8,128)S(1)}, f32[128,24,384]{2,1,0:T(8,128)S(1)}) fusion(bf16[128,384,24]{1,2,0:T(8,128)(2,1)S(1)} %copy.79, bf16[128,384,384]{2,0,1:T(8,128)(2,1)} %all-gather.5.cloned.1.call-done), kind=kOutput, calls=%fused_computation.97 | convolution fusion | flops 907140096 | bytes 44863488 | tf_op jit(solution)/shard_map/cki,ckj->cij/dot_general | solution.py:56
  556.9 0.5 multiply_reduce_fusion
  557.5 0.8 add_convert_fusion
  558.2 0.0 copy-start.2
  558.3 0.8 fusion.38
  559.1 0.8 copy-done.2
  559.9 2.8 fusion.17
  562.7 2.5 copy.83
  (21 shorter events, 0.1 us)
Async XLA Ops:
  6.5 4.2 copy-start.7
  6.5 4.3 copy-start.6
  6.6 4.3 copy-start.5
  6.6 4.3 copy-start.3
  6.6 211.7 %all-gather.3.cloned.1.call-start = ((), (), s32[]{:S(2)}) async-start(), calls=%async_computation.1 | async-start | bytes 40108032 | tf_op jit(solution)/shard_map/all_gather | solution.py:50
  22.3 4.8 copy-start.8
  22.3 4.8 copy-start.9
  22.3 4.8 copy-start.10
  22.3 495.1 %all-gather.5.cloned.1.call-start = ((), (), s32[]{:S(2)}) async-start(), calls=%async_computation.2 | async-start | bytes 40108032 | tf_op jit(solution)/shard_map/all_gather | solution.py:55
  257.3 3.8 copy-start
  260.4 1.5 copy-start.4
  261.9 0.8 copy-start.11
  265.8 3.8 copy-start.1
  558.2 1.7 copy-start.2
Sparse Core Ops, SparseCore 0:
  22.4 195.7 all-gather.2
  277.7 239.6 all-gather.4
where the time goes:
time: 577 us; the launch traced here: 572 us
  waiting for transfers between devices  337 us (58%)
  matrix products  92 us (16%)
  blocking collectives  86.5 us (15%)
  local copies, waits for them, and re-layouts  27.3 us (5%)
  other arithmetic  14.7 us (3%)
  between operations  13.9 us (2%)
    all_gather x2, waiting for transfers between devices, local_layers(): right_all = lax.all_gather(right, 'dap', axis=1, tiled=True)  337 us
    all_to_all x1, blocking collectives, local_layers(): left_cols = lax.all_to_all(left, 'dap', 2, 1, tiled=True)  86.5 us
    dot_general x1, matrix products, local_layers(): jnp.einsum('cki,ckj->cij', left_cols, right_all, preferred_element_type=j...  39.4 us
    dot_general x1, matrix products, local_layers(): jnp.einsum('cik,cjk->cij', left, right_all, preferred_element_type=jnp.fl...  39.1 us
    convert_element_type x4, local copies, waits for them, and re-layouts, gated_side(): (keep_mask * jax.nn.sigmoid(projected[channels:2 * channels]) * projected...  14.5 us
  transfers between devices with their start and end apart: 2, of which 2 were waited for; matrix products, arithmetic and copies ran while one was open for 2% of the time, Pallas kernels for 0%

commit v1 on v0

v1 whole, which is shorter than its diff:
```python
import functools

import jax
import jax.numpy as jnp
from jax import lax
from jax.experimental import pallas as pl
from jax.experimental.pallas import tpu as pltpu
from jax.sharding import PartitionSpec as P

LN_EPS = 1e-5
F32 = jnp.float32
BF16 = jnp.bfloat16
ROWS = 8


def mm(left, right):
    return jnp.dot(left, right, preferred_element_type=F32)


def norm_first(values, scale, offset):
    centred = values - jnp.mean(values, axis=0, keepdims=True)
    variance = jnp.mean(centred * centred, axis=0, keepdims=True)
    return centred * lax.rsqrt(variance + LN_EPS) * scale + offset


def with_bias_row(normed, mask_row):
    width = normed.shape[1]
    first = lax.broadcasted_iota(jnp.int32, (16, width), 0) == 0
    tail = jnp.where(first, jnp.broadcast_to(mask_row, (16, width)), 0.0).astype(BF16)
    zeros = jnp.zeros((112, width), BF16)
    return jnp.concatenate([(normed * mask_row).astype(BF16), tail, zeros], axis=0)


def gated(projected):
    half = projected.shape[0] // 2
    return (jnp.tanh(projected[half:]) + 1.0) * projected[:half]


def spread(store, block, row, values):
    for c in range(store.shape[1]):
        store[block, c, pl.ds(pl.multiple_of(row * 16, 16), 16), :] = values[16 * c:16 * (c + 1)]


def prep_kernel(devices, chunks, z_ref, m_ref, out_ref):
    for q in range(ROWS):
        x = z_ref[q].astype(F32)
        width, channels = x.shape
        x = x.reshape(devices, chunks, ROWS, channels)
        x = jnp.concatenate([x[:, t].reshape(width // chunks, channels) for t in range(chunks)], axis=0)
        out_ref[channels * q:channels * (q + 1), :] = x.T.astype(BF16)
    masks = m_ref[...]
    out_ref[channels * ROWS:, :] = jnp.concatenate([masks, jnp.zeros_like(masks)], axis=0).astype(BF16)


def sides_kernel(core_ref, z_ref, wa_ref, wb_ref, scale_ref, offset_ref, perm_ref,
                 a_ref, b_ref, normed_ref, keep, spread_b, spread_a):
    channels = a_ref.shape[0]
    core = core_ref[0]

    def mask_of(device):
        return z_ref[device, channels * ROWS:channels * ROWS + 2 * ROWS, :].astype(F32)

    def one_b(device, carry):
        masks = mask_of(device)
        for q in range(ROWS):
            x = z_ref[device, channels * q:channels * (q + 1), :].astype(F32)
            normed = norm_first(x, scale_ref[...], offset_ref[...]).astype(BF16)
            keep[device * ROWS + q] = normed
            rhs = with_bias_row(normed.astype(F32), masks[q:q + 1])
            spread(spread_b, device // 2, (device % 2) * ROWS + q, gated(mm(wb_ref[...], rhs)).astype(BF16))
        return carry

    def one_a(chip, carry):
        device = 2 * chip + core
        masks = mask_of(device)
        for q in range(ROWS):
            normed = keep[device * ROWS + q]
            normed_ref[chip * ROWS + q] = normed
            rhs = with_bias_row(normed.astype(F32), masks[q:q + 1])
            spread(spread_a, 0, chip * ROWS + q, gated(mm(wa_ref[...], rhs)).astype(BF16))
        return carry

    lax.fori_loop(0, 4, one_b, 0)
    lax.fori_loop(0, 2, one_a, 0)
    width = b_ref.shape[2]
    for c in range(channels // 16):
        for chip in range(2):
            b_ref[16 * c:16 * (c + 1), 16 * chip:16 * (chip + 1), :] = (
                mm(perm_ref[...], spread_b[chip, c]).reshape(16, 16, width).astype(BF16))
        a_ref[16 * c:16 * (c + 1)] = mm(perm_ref[...], spread_a[0, c]).reshape(16, 16, width).astype(BF16)


def outgoing_kernel(chunks, *refs):
    a_refs, b_refs, o_ref = refs[:chunks], refs[chunks:2 * chunks], refs[-1]
    for c in range(o_ref.shape[0]):
        left = jnp.concatenate([ref[c] for ref in a_refs], axis=0)
        right = jnp.concatenate([ref[c] for ref in b_refs], axis=0)
        o_ref[c] = lax.dot_general(left, right, (((1,), (1,)), ((), ())), preferred_element_type=F32)


def channel_norm(o_ref, scale_ref, offset_ref, store, group):
    channels, rows, width = o_ref.shape

    def load(c):
        return o_ref[pl.ds(c * group, group)]

    total = lax.fori_loop(0, channels // group, lambda c, s: s + jnp.sum(load(c), axis=0),
                          jnp.zeros((rows, width), F32))
    mean = total * (1.0 / channels)

    def square(c, s):
        d = load(c) - mean[None]
        return s + jnp.sum(d * d, axis=0)

    variance = lax.fori_loop(0, channels // group, square, jnp.zeros((rows, width), F32)) * (1.0 / channels)
    scaled = lax.rsqrt(variance + LN_EPS)

    def write(c, carry):
        d = (load(c) - mean[None]) * scaled[None]
        u = d * scale_ref[pl.ds(c * group, group)] + offset_ref[pl.ds(c * group, group)]
        store[c] = u.reshape(group * rows, width).astype(BF16)
        return carry

    lax.fori_loop(0, channels // group, write, 0)


def middle_kernel(place_ref, o_ref, normed_ref, z_ref, no_scale_ref, no_offset_ref, perm_ref, wo_ref, bo_ref, wg_ref, bg_ref,
                  scale_ref, offset_ref, wa_ref, wb_ref, a_ref, b_ref, z1_ref, store, rows_u, spread_a, spread_b):
    channels, rows, width = o_ref.shape
    core, chip = place_ref[0], place_ref[1]
    chips = pl.num_programs(0) * 2
    lanes = 128
    tiles = width // lanes
    channel_norm(o_ref, no_scale_ref, no_offset_ref, store, 16)
    for c in range(channels // 16):
        rows_u[:, 16 * c:16 * (c + 1), :] = mm(perm_ref[...], store[c]).reshape(rows, 16, width).astype(BF16)
    segment = lanes // chips
    lane = lax.broadcasted_iota(jnp.int32, (1, lanes), 1)

    def pick(x):
        parts = []
        for t in range(tiles):
            shift = lax.rem(t * segment - chip * segment + lanes, lanes)
            parts.append(pltpu.roll(x[:, t * lanes:(t + 1) * lanes], shift, 1))
        out = parts[-1]
        for t in reversed(range(tiles - 1)):
            out = jnp.where(lane < (t + 1) * segment, parts[t], out)
        return out

    for half in range(2):
        masks = z_ref[half, 0, channels * ROWS:channels * ROWS + 2 * ROWS, :].astype(F32)
        for q in range(ROWS):
            i = half * ROWS + q
            update = mm(wo_ref[...], rows_u[i]) + bo_ref[...]
            gates = jnp.tanh(mm(wg_ref[...], normed_ref[i]) + bg_ref[...]) + 1.0
            z = z_ref[half, 0, channels * q:channels * (q + 1), :].astype(F32)
            z1 = (z + gates * update).astype(BF16)

            @pl.when(pl.program_id(0) * 2 + half == chip)
            def _():
                z1_ref[q] = z1

            normed = norm_first(z1.astype(F32), scale_ref[...], offset_ref[...]).astype(BF16).astype(F32)
            mask = masks[q:q + 1]
            spread(spread_b, 0, i, gated(mm(wb_ref[...], with_bias_row(normed, mask))).astype(BF16))
            mask_picked = pick(jnp.broadcast_to(mask, (8, width)))[0:1]
            spread(spread_a, 0, i, gated(mm(wa_ref[...], with_bias_row(pick(normed), mask_picked))).astype(BF16))
    for c in range(channels // 16):
        b_ref[16 * c:16 * (c + 1)] = mm(perm_ref[...], spread_b[0, c]).reshape(16, rows, width).astype(BF16)
        a_ref[16 * c:16 * (c + 1)] = mm(perm_ref[...], spread_a[0, c]).reshape(16, rows, lanes).astype(BF16)


def incoming_kernel(chunks, core_ref, *refs):
    a_refs, b_refs, (own_ref, other_ref, whole) = refs[:chunks], refs[chunks:2 * chunks], refs[-3:]
    core = core_ref[0]
    for c in range(own_ref.shape[0]):
        left = jnp.concatenate([ref[c] for ref in a_refs], axis=0)
        right = jnp.concatenate([ref[c] for ref in b_refs], axis=0)
        whole[c] = lax.dot_general(left, right, (((0,), (0,)), ((), ())), preferred_element_type=F32)
        for t in range(chunks):
            rows = pl.ds(t * ROWS, ROWS)
            own_ref[c, rows, :] = whole[c, pl.ds(pl.multiple_of((2 * t + core) * ROWS, ROWS), ROWS), :]
            other_ref[c, rows, :] = whole[c, pl.ds(pl.multiple_of((2 * t + 1 - core) * ROWS, ROWS), ROWS), :]


def last_kernel(devices, own_ref, got_ref, z1_ref, no_scale_ref, no_offset_ref, perm_ref, wo_ref, bo_ref, wg_ref, bg_ref,
                scale_ref, offset_ref, out_ref, total, store, rows_u):
    channels, rows, width = own_ref.shape
    total[...] = own_ref[...] + got_ref[...]
    channel_norm(total, no_scale_ref, no_offset_ref, store, 32)
    for c in range(channels // 32):
        rows_u[:, 32 * c:32 * (c + 1), :] = mm(perm_ref[...], store[c]).reshape(rows, 32, width).astype(BF16)
    chunks = width // (devices * ROWS)
    for q in range(rows):
        z1 = z1_ref[q].astype(F32)
        normed = norm_first(z1, scale_ref[...], offset_ref[...]).astype(BF16)
        update = mm(wo_ref[...], rows_u[q]) + bo_ref[...]
        gates = jnp.tanh(mm(wg_ref[...], normed) + bg_ref[...]) + 1.0
        z2 = (z1 + gates * update).T.reshape(chunks, devices, ROWS, channels)
        z2 = jnp.concatenate([z2[:, d].reshape(chunks * ROWS, channels) for d in range(devices)], axis=0)
        out_ref[q] = z2.astype(BF16)


def spec(block, index):
    return pl.BlockSpec(block, index)


def whole(array):
    return pl.BlockSpec(array.shape, lambda *_: (0,) * array.ndim)


def swap_order(major, minor):
    row = jnp.arange(major * minor)
    source = (row % major) * minor + row // major
    return (source[:, None] == row[None, :]).astype(BF16)


def call(kernel, name, flops, moved, **kw):
    return pl.pallas_call(kernel, name=name,
                          cost_estimate=pl.CostEstimate(flops=flops, bytes_accessed=moved, transcendentals=0),
                          compiler_params=pltpu.CompilerParams(vmem_limit_bytes=60 * 2**20), **kw)


def solution(mesh):
    row_spec = P(("batch", "dap"), None, None)
    mask_spec = P(("batch", "dap"), None)
    devices = mesh.shape["dap"]
    chips = devices // 2

    def local_layers(pair, pair_mask, ln_in, w_proj, b_proj, w_gate, b_gate, ln_out, w_out, b_out):
        mine, width, channels = pair.shape
        chunks = mine // ROWS
        deep = channels * ROWS + 2 * ROWS
        index = lax.axis_index("dap")
        core, chip = lax.rem(index, 2), index // 2
        place = jnp.stack([core, chip]).astype(jnp.int32)

        mask = pair_mask.astype(F32).reshape(mine, devices, chunks, ROWS).transpose(0, 2, 1, 3).reshape(mine, width)
        packed = []
        for t in range(chunks):
            packed.append(call(
                functools.partial(prep_kernel, devices, chunks), "prep", 10**6, 10**6,
                grid=(1,),
                in_specs=[spec((ROWS, width, channels), lambda s, t=t: (t, 0, 0)), spec((ROWS, width), lambda s, t=t: (t, 0))],
                out_specs=spec((deep, width), lambda s: (0, 0)),
                out_shape=jax.ShapeDtypeStruct((deep, width), BF16))(pair, mask))
        gathered = [lax.all_gather(part, "dap", axis=0, tiled=True).reshape(devices, deep, width) for part in packed]

        def lanes(vector):
            return jnp.broadcast_to(vector.astype(F32)[:, None], (channels, width))

        def planes(vector):
            return jnp.broadcast_to(vector.astype(F32)[:, None, None], (channels, 1, width))

        def side(layer, at):
            w = w_proj[layer][:, 2 * at * channels:2 * (at + 1) * channels].T * BF16(0.5)
            bias = b_proj[layer][2 * at * channels:2 * (at + 1) * channels, None] * BF16(0.5)
            return jnp.concatenate([w, bias, jnp.zeros((2 * channels, channels - 1), BF16)], axis=1)

        wa = [side(layer, 0) for layer in range(2)]
        wb = [side(layer, 1) for layer in range(2)]
        wo = [w_out[layer].T * BF16(0.5) for layer in range(2)]
        wg = [w_gate[layer].T * BF16(0.5) for layer in range(2)]
        bo = [lanes(b_out[layer]) * 0.5 for layer in range(2)]
        bg = [lanes(b_gate[layer]) * 0.5 for layer in range(2)]
        scale_in = [lanes(ln_in[layer, 0]) for layer in range(2)]
        offset_in = [lanes(ln_in[layer, 1]) for layer in range(2)]
        scale_out = [planes(ln_out[layer, 0]) for layer in range(2)]
        offset_out = [planes(ln_out[layer, 1]) for layer in range(2)]
        perm16 = swap_order(16, 16)
        perm_last = swap_order(32, 8)

        chunk_rows = devices * ROWS
        half_rows = chips * ROWS
        steps = devices // 4
        a1, b1, normed1 = [], [], []
        for t in range(chunks):
            consts = [wa[0], wb[0], scale_in[0], offset_in[0], perm16]
            a, b, n = call(
                sides_kernel, "sides", 10**10, 10**8,
                grid_spec=pltpu.PrefetchScalarGridSpec(
                    num_scalar_prefetch=1, grid=(steps,),
                    in_specs=[spec((4, deep, width), lambda s, *_: (s, 0, 0))] + [whole(x) for x in consts],
                    out_specs=[spec((channels, 2 * ROWS, width), lambda s, *_: (0, s, 0)),
                               spec((channels, 4 * ROWS, width), lambda s, *_: (0, s, 0)),
                               spec((2 * ROWS, channels, width), lambda s, *_: (s, 0, 0))],
                    scratch_shapes=[pltpu.VMEM((4 * ROWS, channels, width), BF16),
                                    pltpu.VMEM((2, channels // 16, 256, width), BF16),
                                    pltpu.VMEM((1, channels // 16, 256, width), BF16)]),
                out_shape=[jax.ShapeDtypeStruct((channels, half_rows, width), BF16),
                           jax.ShapeDtypeStruct((channels, chunk_rows, width), BF16),
                           jax.ShapeDtypeStruct((half_rows, channels, width), BF16)])(place, gathered[t], *consts)
            a1.append(a)
            b1.append(b)
            normed1.append(n)

        some = 4
        o1 = call(
            functools.partial(outgoing_kernel, chunks), "outgoing", 10**10, 10**8,
            grid=(channels // some,),
            in_specs=[spec((some, half_rows, width), lambda s: (s, 0, 0))] * chunks
            + [spec((some, chunk_rows, width), lambda s: (s, 0, 0))] * chunks,
            out_specs=spec((some, chunks * half_rows, width), lambda s: (s, 0, 0)),
            out_shape=jax.ShapeDtypeStruct((channels, chunks * half_rows, width), F32))(*a1, *b1)

        a2, b2, z1 = [], [], []
        steps = half_rows // 16
        for t in range(chunks):
            consts = [scale_out[0], offset_out[0], perm16, wo[0], bo[0], wg[0], bg[0],
                      scale_in[1], offset_in[1], wa[1], wb[1]]
            by_core = gathered[t].reshape(chips, 2, deep, width)
            a, b, z = call(
                middle_kernel, "middle", 10**10, 10**8,
                grid_spec=pltpu.PrefetchScalarGridSpec(
                    num_scalar_prefetch=1, grid=(steps,),
                    in_specs=[spec((channels, 16, width), lambda s, place, t=t: (0, t * steps + s, 0)),
                              spec((16, channels, width), lambda s, place: (s, 0, 0)),
                              spec((2, 1, deep, width), lambda s, place: (s, place[0], 0, 0))]
                    + [whole(x) for x in consts],
                    out_specs=[spec((channels, 16, 128), lambda s, *_: (0, s, 0)),
                               spec((channels, 16, width), lambda s, *_: (0, s, 0)),
                               spec((ROWS, channels, width), lambda s, *_: (0, 0, 0))],
                    scratch_shapes=[pltpu.VMEM((channels // 16, 256, width), BF16),
                                    pltpu.VMEM((16, channels, width), BF16),
                                    pltpu.VMEM((1, channels // 16, 256, 128), BF16),
                                    pltpu.VMEM((1, channels // 16, 256, width), BF16)]),
                out_shape=[jax.ShapeDtypeStruct((channels, half_rows, 128), BF16),
                           jax.ShapeDtypeStruct((channels, half_rows, width), BF16),
                           jax.ShapeDtypeStruct((ROWS, channels, width), BF16)])(place, o1, normed1[t], by_core, *consts)
            a2.append(a)
            b2.append(b)
            z1.append(z)

        some = 8
        own, other = call(
            functools.partial(incoming_kernel, chunks), "incoming", 10**10, 10**8,
            grid_spec=pltpu.PrefetchScalarGridSpec(
                num_scalar_prefetch=1, grid=(channels // some,),
                in_specs=[spec((some, half_rows, 128), lambda s, *_: (s, 0, 0))] * chunks
                + [spec((some, half_rows, width), lambda s, *_: (s, 0, 0))] * chunks,
                out_specs=[spec((some, mine, width), lambda s, *_: (s, 0, 0))] * 2,
                scratch_shapes=[pltpu.VMEM((some, 128, width), F32)]),
            out_shape=[jax.ShapeDtypeStruct((channels, mine, width), F32)] * 2)(place, *a2, *b2)
        got = lax.ppermute(other, "dap", [(d, d ^ 1) for d in range(devices)])

        consts = [scale_out[1], offset_out[1], perm_last, wo[1], bo[1], wg[1], bg[1], scale_in[1], offset_in[1]]
        z1 = jnp.concatenate(z1, axis=0)
        return call(
            functools.partial(last_kernel, devices), "last", 10**9, 10**7,
            grid=(chunks,),
            in_specs=[spec((channels, ROWS, width), lambda s: (0, s, 0))] * 2
            + [spec((ROWS, channels, width), lambda s: (s, 0, 0))] + [whole(x) for x in consts],
            out_specs=spec((ROWS, width, channels), lambda s: (s, 0, 0)),
            out_shape=jax.ShapeDtypeStruct(pair.shape, BF16),
            scratch_shapes=[pltpu.VMEM((channels, ROWS, width), F32),
                            pltpu.VMEM((channels // 32, 256, width), BF16),
                            pltpu.VMEM((ROWS, channels, width), BF16)])(own, got, z1, *consts)

    return jax.shard_map(local_layers, mesh=mesh,
                         in_specs=(row_spec, mask_spec, P(), P(), P(), P(), P(), P(), P(), P()),
                         out_specs=row_spec, check_vma=False)
```

time: 577 us -> 510 us (0.88)
  Pallas kernels: 0 us -> 331 us
  waiting for transfers between devices: 337 us -> 142 us
  matrix products: 92 us -> 0 us
  blocking collectives: 86.5 us -> 0 us
  local copies, waits for them, and re-layouts: 27.3 us -> 12.7 us
  other arithmetic: 14.7 us -> 6.07 us
    pallas_call x0 -> x12, Pallas kernels: none -> 331 us  [the longest x3 131 us: local_layers(): call(middle_kernel, 'middle', 10 ** 10, 10 ** 8, grid_spec=pltpu.Prefetch...]
    all_gather x2 -> x3, waiting for transfers between devices: 337 us -> 138 us  [local_layers(): lax.all_gather(part, 'dap', axis=0, tiled=True)]
    dot_general x8 -> x0, matrix products: 92 us -> none  [the longest x1 39.4 us: local_layers(): jnp.einsum('cki,ckj->cij', left_cols, right_all, preferred_element_type=j...]
    all_to_all x1 -> x0, blocking collectives: 86.5 us -> none  [local_layers(): left_cols = lax.all_to_all(left, 'dap', 2, 1, tiled=True)]
    convert_element_type x5 -> x0, local copies, waits for them, and re-layouts: 17 us -> none  [the longest x4 14.5 us: gated_side(): (keep_mask * jax.nn.sigmoid(projected[channels:2 * channels]) * projected...]
    broadcast_in_dim x0 -> x12, local copies, waits for them, and re-layouts: none -> 9.59 us  [the longest x8 6.05 us: lanes(): return jnp.broadcast_to(vector.astype(F32)[:, None], (channels, width))]
    convert_element_type x8 -> x5, other arithmetic: 9.37 us -> 1.52 us  [the longest x2 1.49 us: swap_order(): return (source[:, None] == row[None, :]).astype(BF16)]
  transfers between devices with their start and end apart: 2 -> 4, of which waited for: 2 -> 4; matrix products, arithmetic and copies ran while one was open for 2% -> 2% of each run, Pallas kernels for 0% -> 16%
where the time goes in v1:
time: 510 us; the launch traced here: 506 us
  Pallas kernels  331 us (65%)
  waiting for transfers between devices  142 us (28%)
  between operations  13.7 us (3%)
  local copies, waits for them, and re-layouts  12.7 us (2%)
  other arithmetic  6.07 us (1%)
    all_gather x3, waiting for transfers between devices, local_layers(): lax.all_gather(part, 'dap', axis=0, tiled=True)  138 us
    pallas_call x3, Pallas kernels, local_layers(): call(middle_kernel, 'middle', 10 ** 10, 10 ** 8, grid_spec=pltpu.Prefetch...  131 us
    pallas_call x3, Pallas kernels, local_layers(): call(sides_kernel, 'sides', 10 ** 10, 10 ** 8, grid_spec=pltpu.PrefetchSc...  115 us
    pallas_call x1, Pallas kernels, local_layers(): call(functools.partial(outgoing_kernel, chunks), 'outgoing', 10 ** 10, 10...  47.5 us
    pallas_call x1, Pallas kernels, local_layers(): call(functools.partial(incoming_kernel, chunks), 'incoming', 10 ** 10, 10...  20.2 us
    pallas_call x1, Pallas kernels, local_layers(): call(functools.partial(last_kernel, devices), 'last', 10 ** 9, 10 ** 7, g...  10.6 us
  transfers between devices with their start and end apart: 4, of which 4 were waited for; matrix products, arithmetic and copies ran while one was open for 2% of the time, Pallas kernels for 16%

profile of v1, /device:TPU:21, one launch (start us, length us, event | category | flops | bytes accessed | tf_op | source)
XLA Modules:
  0.0 506.3 jit_solution(9517610639404705427)
XLA Ops:
  6.6 0.9 copy.18
  7.5 0.7 copy.20.m_ref
  8.3 2.4 prep.4
  10.8 2.3 prep.5
  13.3 2.3 prep.3
  15.7 0.1 copy.36
  15.8 0.1 copy.33
  16.0 0.1 copy.22
  16.1 0.1 copy.23
  16.3 0.1 copy.29
  16.4 0.1 copy.30
  16.6 0.1 copy.34
  16.7 0.1 copy.35
  17.0 0.6 pad_add_fusion.core_ref.place_ref
  17.7 0.6 multiply_bitcast_fusion.2
  18.3 0.7 fusion.perm_ref
  19.1 0.9 maximum_maximum_fusion.3
  20.0 69.1 %all-gather.6.cloned.1.call-done = bf16[16640,384]{1,0:T(8,128)(2,1)} async-done(((bf16[1040,384]{1,0:T(8,128)(2,1)}), bf16[16640,384]{1,0:T(8,128)(2,1)}) %all-gather.6.cloned.1.call-update) | async-done | bytes 12779536 | tf_op jit(solution)/shard_map/all_gather | solution.py:247
  89.1 0.8 broadcast_in_dim.24.scale_ref
  89.8 0.8 broadcast_in_dim.25.offset_ref
  90.6 38.6 %sides.4 = (bf16[128,64,384]{2,1,0:T(8,128)(2,1)}, bf16[128,128,384]{2,1,0:T(8,128)(2,1)}, bf16[64,128,384]{2,1,0:T(8,128)(2,1)}) custom-call(s32[2]{0:T(128)} %pad_add_fusion.core_ref.place_ref, bf16[16,1040,384]{2,1,0:T(8,128)(2,1)} %bitcast.78, bf16[256,256]{1,0:T(8,128)(2,1)} %get-tuple-element.74.wa_ref, bf16[256,256]{1,0:T(8,128)(2,1)} %get-tuple-element.72.wb_ref, ...), custom_call_target="tpu_custom_call" | custom-call | flops 10000000000 | bytes 100000000 | tf_op jit(solution)/shard_map/sides/pallas_call | solution.py:279
  129.2 33.3 %all-gather.8.cloned.1.call-done = bf16[16640,384]{1,0:T(8,128)(2,1)} async-done(((bf16[1040,384]{1,0:T(8,128)(2,1)}), bf16[16640,384]{1,0:T(8,128)(2,1)}) %all-gather.8.cloned.1.call-update) | async-done | bytes 12779536 | tf_op jit(solution)/shard_map/all_gather | solution.py:247
  162.4 38.1 %sides.5 = (bf16[128,64,384]{2,1,0:T(8,128)(2,1)}, bf16[128,128,384]{2,1,0:T(8,128)(2,1)}, bf16[64,128,384]{2,1,0:T(8,128)(2,1)}) custom-call(s32[2]{0:T(128)} %pad_add_fusion.core_ref.place_ref, bf16[16,1040,384]{2,1,0:T(8,128)(2,1)} %bitcast.82, bf16[256,256]{1,0:T(8,128)(2,1)} %get-tuple-element.74.wa_ref, bf16[256,256]{1,0:T(8,128)(2,1)} %get-tuple-element.72.wb_ref, ...), custom_call_target="tpu_custom_call" | custom-call | flops 10000000000 | bytes 100000000 | tf_op jit(solution)/shard_map/sides/pallas_call | solution.py:279
  200.5 35.3 %all-gather.4.cloned.1.call-done = bf16[16640,384]{1,0:T(8,128)(2,1)} async-done(((bf16[1040,384]{1,0:T(8,128)(2,1)}), bf16[16640,384]{1,0:T(8,128)(2,1)}) %all-gather.4.cloned.1.call-update) | async-done | bytes 12779536 | tf_op jit(solution)/shard_map/all_gather | solution.py:247
  235.8 38.1 %sides.3 = (bf16[128,64,384]{2,1,0:T(8,128)(2,1)}, bf16[128,128,384]{2,1,0:T(8,128)(2,1)}, bf16[64,128,384]{2,1,0:T(8,128)(2,1)}) custom-call(s32[2]{0:T(128)} %pad_add_fusion.core_ref.place_ref, bf16[16,1040,384]{2,1,0:T(8,128)(2,1)} %bitcast.80, bf16[256,256]{1,0:T(8,128)(2,1)} %get-tuple-element.74.wa_ref, bf16[256,256]{1,0:T(8,128)(2,1)} %get-tuple-element.72.wb_ref, ...), custom_call_target="tpu_custom_call" | custom-call | flops 10000000000 | bytes 100000000 | tf_op jit(solution)/shard_map/sides/pallas_call | solution.py:279
  273.9 47.5 %outgoing.1.o_ref = f32[128,192,384]{2,1,0:T(8,128)} custom-call(bf16[128,64,384]{2,1,0:T(8,128)(2,1)} %get-tuple-element.25.refs_0_, bf16[128,64,384]{2,1,0:T(8,128)(2,1)} %get-tuple-element.26.refs_1_, bf16[128,64,384]{2,1,0:T(8,128)(2,1)} %get-tuple-element.27.refs_2_, bf16[128,128,384]{2,1,0:T(8,128)(2,1)} %get-tuple-element.28.refs_3_, ...), custom_call_target="tpu_custom_call" | custom-call | flops 10000000000 | bytes 100000000 | tf_op jit(solution)/shard_map/outgoing/pallas_call | solution.py:298
  321.4 0.8 broadcast_in_dim.30.scale_ref
  322.2 0.8 broadcast_in_dim.31.offset_ref
  323.0 0.9 broadcast_in_dim.26.no_scale_ref
  323.8 0.9 broadcast_in_dim.27.no_offset_ref
  324.7 0.7 broadcast_in_dim.28.bo_ref
  325.5 0.8 broadcast_in_dim.29.bg_ref
  326.2 43.7 %middle.5 = (bf16[128,64,128]{2,1,0:T(8,128)(2,1)}, bf16[128,64,384]{2,1,0:T(8,128)(2,1)}, bf16[8,128,384]{2,1,0:T(8,128)(2,1)}) custom-call(s32[2]{0:T(128)} %pad_add_fusion.core_ref.place_ref, f32[128,192,384]{2,1,0:T(8,128)} %outgoing.1.o_ref, bf16[64,128,384]{2,1,0:T(8,128)(2,1)} %get-tuple-element.35.normed_ref, bf16[8,2,1040,384]{3,2,1,0:T(8,128)(2,1)} %bitcast.83, ...), custom_call_target="tpu_custom_call" | custom-call | flops 10000000000 | bytes 100000000 | tf_op jit(solution)/shard_map/middle/pallas_call | solution.py:312
  369.9 43.7 %middle.4 = (bf16[128,64,128]{2,1,0:T(8,128)(2,1)}, bf16[128,64,384]{2,1,0:T(8,128)(2,1)}, bf16[8,128,384]{2,1,0:T(8,128)(2,1)}) custom-call(s32[2]{0:T(128)} %pad_add_fusion.core_ref.place_ref, f32[128,192,384]{2,1,0:T(8,128)} %outgoing.1.o_ref, bf16[64,128,384]{2,1,0:T(8,128)(2,1)} %get-tuple-element.33.normed_ref, bf16[8,2,1040,384]{3,2,1,0:T(8,128)(2,1)} %bitcast.79, ...), custom_call_target="tpu_custom_call" | custom-call | flops 10000000000 | bytes 100000000 | tf_op jit(solution)/shard_map/middle/pallas_call | solution.py:312
  413.6 43.9 %middle.3 = (bf16[128,64,128]{2,1,0:T(8,128)(2,1)}, bf16[128,64,384]{2,1,0:T(8,128)(2,1)}, bf16[8,128,384]{2,1,0:T(8,128)(2,1)}) custom-call(s32[2]{0:T(128)} %pad_add_fusion.core_ref.place_ref, f32[128,192,384]{2,1,0:T(8,128)} %outgoing.1.o_ref, bf16[64,128,384]{2,1,0:T(8,128)(2,1)} %get-tuple-element.31.normed_ref, bf16[8,2,1040,384]{3,2,1,0:T(8,128)(2,1)} %bitcast.81, ...), custom_call_target="tpu_custom_call" | custom-call | flops 10000000000 | bytes 100000000 | tf_op jit(solution)/shard_map/middle/pallas_call | solution.py:312
  457.5 20.2 %incoming.1 = (f32[128,24,384]{2,1,0:T(8,128)}, f32[128,24,384]{2,1,0:T(8,128)}) custom-call(s32[2]{0:T(128)} %pad_add_fusion.core_ref.place_ref, bf16[128,64,128]{2,1,0:T(8,128)(2,1)} %get-tuple-element.32.refs_0_, bf16[128,64,128]{2,1,0:T(8,128)(2,1)} %get-tuple-element.34.refs_1_, bf16[128,64,128]{2,1,0:T(8,128)(2,1)} %get-tuple-element.36.refs_2_, ...), custom_call_target="tpu_custom_call" | custom-call | flops 10000000000 | bytes 100000000 | tf_op jit(solution)/shard_map/incoming/pallas_call | solution.py:335
  477.7 0.3 collective-permute-start
  478.0 0.1 copy.37
  478.2 0.1 copy.38
  478.3 0.6 multiply_bitcast_fusion
  478.9 0.8 fusion.1.perm_ref
  479.7 1.7 pad_maximum_fusion.z1_ref
  481.4 4.2 collective-permute-done.got_ref
  485.6 0.9 broadcast_in_dim.32.no_scale_ref
  486.5 0.9 broadcast_in_dim.33.no_offset_ref
  487.3 0.8 broadcast_in_dim.34.bo_ref
  488.1 0.8 broadcast_in_dim.35.bg_ref
  488.9 10.6 %last.1 = bf16[24,384,128]{2,1,0:T(8,128)(2,1)} custom-call(f32[128,24,384]{2,1,0:T(8,128)} %get-tuple-element.40.own_ref, f32[128,24,384]{2,1,0:T(8,128)} %collective-permute-done.got_ref, bf16[24,128,384]{2,1,0:T(8,128)(2,1)} %pad_maximum_fusion.z1_ref, f32[128,1,384]{2,1,0:T(1,128)} %broadcast_in_dim.32.no_scale_ref, ...), custom_call_target="tpu_custom_call" | custom-call | flops 1000000000 | bytes 10000000 | tf_op jit(solution)/shard_map/last/pallas_call | solution.py:348
  (43 shorter events, 0.6 us)
Async XLA Ops:
  6.5 82.5 %all-gather.6.cloned.1.call-start = ((), (), s32[]{:S(2)}) async-start(), calls=%async_computation.1 | async-start | bytes 13578240 | tf_op jit(solution)/shard_map/all_gather | solution.py:247
  7.5 8.2 %copy-start.3 = (bf16[2,128,512]{2,1,0:T(8,128)(2,1)S(1)}, bf16[2,128,512]{2,1,0:T(8,128)(2,1)}, u32[]{:S(2)}) copy-start(bf16[2,128,512]{2,1,0:T(8,128)(2,1)} %param.13) | copy-start | bytes 786436
  8.2 7.7 %copy-start.6 = (bf16[2,512]{1,0:T(2,128)(2,1)S(1)}, bf16[2,512]{1,0:T(2,128)(2,1)}, u32[]{:S(2)}) copy-start(bf16[2,512]{1,0:T(2,128)(2,1)} %param.14) | copy-start | bytes 6148
  8.2 8.3 %copy-start.4 = (bf16[2,128,128]{2,1,0:T(8,128)(2,1)S(1)}, bf16[2,128,128]{2,1,0:T(8,128)(2,1)}, u32[]{:S(2)}) copy-start(bf16[2,128,128]{2,1,0:T(8,128)(2,1)} %param.18) | copy-start | bytes 196612
  8.2 8.5 %copy-start.5 = (bf16[2,128,128]{2,1,0:T(8,128)(2,1)S(1)}, bf16[2,128,128]{2,1,0:T(8,128)(2,1)}, u32[]{:S(2)}) copy-start(bf16[2,128,128]{2,1,0:T(8,128)(2,1)} %param.15) | copy-start | bytes 196612
  8.2 9.4 %copy-start.9 = (bf16[2,128]{1,0:T(2,128)(2,1)S(1)}, bf16[2,128]{1,0:T(2,128)(2,1)}, u32[]{:S(2)}) copy-start(bf16[2,128]{1,0:T(2,128)(2,1)} %param.19) | copy-start | bytes 1540
  8.2 9.4 %copy-start.10 = (bf16[2,128]{1,0:T(2,128)(2,1)S(1)}, bf16[2,128]{1,0:T(2,128)(2,1)}, u32[]{:S(2)}) copy-start(bf16[2,128]{1,0:T(2,128)(2,1)} %param.16) | copy-start | bytes 1540
  8.2 9.4 %copy-start.7 = (bf16[2,2,128]{2,1,0:T(2,128)(2,1)S(1)}, bf16[2,2,128]{2,1,0:T(2,128)(2,1)}, u32[]{:S(2)}) copy-start(bf16[2,2,128]{2,1,0:T(2,128)(2,1)} %param.12) | copy-start | bytes 3076
  8.3 9.4 %copy-start.8 = (bf16[2,2,128]{2,1,0:T(2,128)(2,1)S(1)}, bf16[2,2,128]{2,1,0:T(2,128)(2,1)}, u32[]{:S(2)}) copy-start(bf16[2,2,128]{2,1,0:T(2,128)(2,1)} %param.17) | copy-start | bytes 3076
  10.7 151.7 %all-gather.8.cloned.1.call-start = ((), (), s32[]{:S(2)}) async-start(), calls=%async_computation.2 | async-start | bytes 13578240 | tf_op jit(solution)/shard_map/all_gather | solution.py:247
  13.2 222.6 %all-gather.4.cloned.1.call-start = ((), (), s32[]{:S(2)}) async-start(), calls=%async_computation | async-start | bytes 13578240 | tf_op jit(solution)/shard_map/all_gather | solution.py:247
  457.5 22.2 %copy-start = (bf16[8,128,384]{2,1,0:T(8,128)(2,1)S(1)}, bf16[8,128,384]{2,1,0:T(8,128)(2,1)}, u32[]{:S(2)}) copy-start(bf16[8,128,384]{2,1,0:T(8,128)(2,1)} %get-tuple-element.44) | copy-start | bytes 2359300
  457.5 22.2 %copy-start.1 = (bf16[8,128,384]{2,1,0:T(8,128)(2,1)S(1)}, bf16[8,128,384]{2,1,0:T(8,128)(2,1)}, u32[]{:S(2)}) copy-start(bf16[8,128,384]{2,1,0:T(8,128)(2,1)} %get-tuple-element.43) | copy-start | bytes 2359300
  457.5 22.2 %copy-start.2 = (bf16[8,128,384]{2,1,0:T(8,128)(2,1)S(1)}, bf16[8,128,384]{2,1,0:T(8,128)(2,1)}, u32[]{:S(2)}) copy-start(bf16[8,128,384]{2,1,0:T(8,128)(2,1)} %get-tuple-element.42) | copy-start | bytes 2359300
  477.7 7.9 %collective-permute-start = (f32[128,24,384]{2,1,0:T(8,128)}, f32[128,24,384]{2,1,0:T(8,128)}, u32[]{:S(2)}, u32[]{:S(2)}) collective-permute-start(f32[128,24,384]{2,1,0:T(8,128)} %get-tuple-element.41), channel_id=1, source_target_pairs={{0,1},{1,0},{2,3},{3,2},{4,5},{5,4},{6,7},{7,6},{8,9},{9,8},{10,11... | collective-permute-start | bytes 14155784 | tf_op jit(solution)/shard_map/ppermute | solution.py:344
Sparse Core Ops, SparseCore 0:
  10.8 78.1 all-gather.5
  90.7 71.6 all-gather.7
  164.1 71.6 all-gather.3
